TPU v7x, 256 devices: a whole 4x4x8 slice. The times are simulated.
256 devices in a mesh: heads: 4 (over y_hi, core), blk: 64 (over y_lo, z, x).
Axes of the slice: x: 4, y: 4 (y_hi: 2, y_lo: 2; y = y_hi * 2 + y_lo), z: 8, core: 2. Of those that a mesh axis runs over, the one named last changes fastest.
Arguments:
- tokens: bfloat16 [32768, 4096], P(('blk', 'heads')), may hold values from -6 to 6
- w_query: bfloat16 [4096, 2048], P('blk', 'heads'), may hold values from -0.75 to 0.75
- key_value_weight: bfloat16 [4096, 2, 512], P('blk', None, 'heads'), may hold values from -0.75 to 0.75
- w_out: bfloat16 [2048, 4096], P(('heads', 'blk')), may hold values from -0.5 to 0.5
- doc_lengths: int32 [16], replicated, may hold values from 1 to 8192, 32768 in all
Outputs:
- attended: bfloat16 [32768, 4096], P(('blk', 'heads'))
Inputs may be any that keep to these rules, and one draw needn't show every extreme that they name: `doc_lengths`: the 16 lengths sum to 32768; the longest document has exactly 8192 tokens.
All inputs are finite; a program needn't handle non-finite values.
Results may differ from a plain program's by a relative error of at most 0.012.
Values may be sent and summed in bfloat16 or wider, within the bound.
A program may use at most 128 MiB of HBM per device.

v0:
```python
import jax
import jax.numpy as jnp
from jax import lax
from jax.sharding import PartitionSpec as P

HEAD_SIZE = 128
norm_epsilon = 1e-05
rope_base = 500000.0
masked_score = -1e30


def in_one_piece(arrays, axis, dim, along):
    columns = [a.reshape(*a.shape[:along], -1) for a in arrays]
    both = jnp.concatenate(columns, axis=along)
    whole, at, finished = (lax.all_gather(both, axis, axis=dim, tiled=True), 0, [])
    for a, column in zip(arrays, columns):
        piece = whole[..., at : at + column.shape[along]]
        finished.append(piece.reshape(*piece.shape[:along], *a.shape[along:]))
        at += column.shape[along]
    return tuple(finished)


def shifted(value, axis, steps):
    count = lax.axis_size(axis)
    first, last = (max(0, -steps), min(count, count - steps))
    return lax.ppermute(value, axis, [(source, source + steps) for source in range(first, last)])


def locate_documents(positions, doc_lengths):
    ends = jnp.cumsum(doc_lengths)
    after = positions[:, None] >= ends[None, :]
    ident = jnp.sum(after.astype(jnp.int32), axis=1)
    starts = jnp.sum(jnp.where(after, doc_lengths[None, :], 0), axis=1)
    return (ident, starts)


def apply_rotation(values, relative_offset):
    half = values.shape[-1] // 2
    freqs = jnp.power(rope_base, -2.0 * jnp.arange(half, dtype=jnp.float32) / values.shape[-1])
    angle = relative_offset.astype(jnp.float32)[:, None] * freqs[None, :]
    cosine = jnp.cos(angle)[:, None, :]
    sine = jnp.sin(angle)[:, None, :]
    first = values[..., :half]
    second = values[..., half:]
    return jnp.concatenate(
        [first * cosine - second * sine, second * cosine + first * sine], axis=-1
    )


def on_device(tokens, w_query, key_value_weight, w_out, doc_lengths):
    blk_index = lax.axis_index("blk")
    reach = lax.axis_size("blk") // 4
    values = tokens.astype(jnp.float32)
    normalized_input = (
        values * lax.rsqrt(jnp.mean(values * values, axis=1, keepdims=True) + norm_epsilon)
    ).astype(jnp.bfloat16)
    block_input = lax.all_gather(normalized_input, "heads", axis=0, tiled=True)
    block_rows = block_input.shape[0]
    query_cols = w_query.shape[1]
    kv_cols = key_value_weight.shape[2]
    pieces = in_one_piece((w_query, key_value_weight), "blk", 0, 1)
    count = pieces[0].shape[0]
    query_part = jnp.dot(block_input, pieces[0], preferred_element_type=jnp.float32)
    keyval_part = jnp.dot(
        block_input, pieces[1].reshape(count, 2 * kv_cols), preferred_element_type=jnp.float32
    )
    positions = blk_index * block_rows + jnp.arange(block_rows, dtype=jnp.int32)
    ident, starts = locate_documents(positions, doc_lengths)
    relative_offset = positions - starts
    query_heads = query_cols // HEAD_SIZE
    kv_heads = kv_cols // HEAD_SIZE
    head_group = query_heads // kv_heads
    query_rows = apply_rotation(
        query_part.reshape(block_rows, query_heads, HEAD_SIZE), relative_offset
    ).astype(jnp.bfloat16)
    query_rows = query_rows.reshape(block_rows, kv_heads, head_group, HEAD_SIZE)
    rotated_keys = apply_rotation(
        keyval_part[:, :kv_cols].reshape(block_rows, kv_heads, HEAD_SIZE), relative_offset
    ).astype(jnp.bfloat16)
    value_rows = (
        keyval_part[:, kv_cols:].reshape(block_rows, kv_heads, HEAD_SIZE).astype(jnp.bfloat16)
    )
    kv_block = jnp.stack([rotated_keys, value_rows], axis=1)
    scale = HEAD_SIZE ** (-0.5)

    def attend_tile(state, kv_now, distance):
        key_pos = (blk_index - distance) * block_rows + jnp.arange(block_rows, dtype=jnp.int32)
        key_doc, unused_k = locate_documents(key_pos, doc_lengths)
        keep = (
            (key_pos[None, :] >= 0)
            & (key_pos[None, :] <= positions[:, None])
            & (key_doc[None, :] == ident[:, None])
        )
        highest, totals, accum = state
        scores = (
            jnp.einsum(
                "qhgd,khd->hgqk", query_rows, kv_now[:, 0], preferred_element_type=jnp.float32
            )
            * scale
        )
        scores = jnp.where(keep, scores, masked_score)
        new_high = jnp.maximum(highest, jnp.max(scores, axis=-1))
        fading = jnp.exp(highest - new_high)
        probs = jnp.where(keep, jnp.exp(scores - new_high[..., None]), 0.0)
        totals = totals * fading + jnp.sum(probs, axis=-1)
        update = jnp.einsum(
            "hgqk,khd->hgqd",
            probs.astype(jnp.bfloat16),
            kv_now[:, 1],
            preferred_element_type=jnp.float32,
        )
        accum = accum * fading[..., None] + update
        return (new_high, totals, accum)

    initial = (
        jnp.full((kv_heads, head_group, block_rows), masked_score, jnp.float32),
        jnp.zeros((kv_heads, head_group, block_rows), jnp.float32),
        jnp.zeros((kv_heads, head_group, block_rows, HEAD_SIZE), jnp.float32),
    )
    state = attend_tile(initial, kv_block, 0)

    def advance(distance, carry):
        kv_now, inner = carry
        kv_now = shifted(kv_now, "blk", 1)
        return (kv_now, attend_tile(inner, kv_now, distance))

    unused_kv, state = lax.fori_loop(1, reach + 1, advance, (kv_block, state))
    highest, totals, accum = state
    mixed = accum / totals[..., None]
    mixed = mixed.transpose(2, 0, 1, 3).reshape(block_rows, query_cols).astype(jnp.bfloat16)
    head_rows = lax.all_gather(w_out, "blk", axis=0, tiled=True)
    return lax.psum_scatter(
        jnp.dot(mixed, head_rows, preferred_element_type=jnp.float32).astype(jnp.bfloat16),
        "heads",
        scatter_dimension=0,
        tiled=True,
    )


def solution(mesh):
    return jax.shard_map(
        on_device,
        mesh=mesh,
        in_specs=(
            P(("blk", "heads"), None),
            P("blk", "heads"),
            P("blk", None, "heads"),
            P(("heads", "blk"), None),
            P(),
        ),
        out_specs=P(("blk", "heads"), None),
        check_vma=False,
    )
```

profile of v0, /device:TPU:1, one launch (start us, length us, event | category | flops | bytes accessed | tf_op | source)
XLA Modules:
  0.0 733.6 jit_solution(8738411729264827400)
XLA Ops:
  13.8 42.2 %all-gather.4.cloned.1.call-done = bf16[512,4096]{1,0:T(8,128)(2,1)} async-done(((bf16[128,4096]{1,0:T(8,128)(2,1)}), bf16[512,4096]{1,0:T(8,128)(2,1)}) %all-gather.4.cloned.1.call-update) | async-done | bytes 4194320 | tf_op jit(solution)/shard_map/all_gather | solution.py:57
  56.0 262.9 %all-gather.6.cloned.1.call-done = bf16[4096,768]{1,0:T(8,128)(2,1)} async-done(((bf16[64,768]{1,0:T(8,128)(2,1)}), bf16[4096,768]{1,0:T(8,128)(2,1)}) %all-gather.6.cloned.1.call-update) | async-done | bytes 6291472 | tf_op jit(solution)/shard_map/all_gather | solution.py:15
  318.9 4.2 fusion.29
  324.8 5.8 fusion.21
  335.9 211.9 %while.22 = (s32[]{:T(128)}, bf16[512,2,1,128]{3,0,2,1:T(8,128)(2,1)S(1)}, f32[1,4,512]{2,1,0:T(4,128)S(1)}, f32[1,4,512]{2,1,0:T(4,128)S(1)}, f32[1,4,512,128]{...) while((s32[]{:T(128)}, ...), condition=%wide.region_10.11_spmd.clone, body=%wide.region_6.10_spmd.clone.sunk | while | flops 552107520 | bytes 18236672 | solution.py:127
  345.7 4.2 collective-permute-start
  384.4 6.1 collective-permute-done
  398.7 6.4 collective-permute-done
  409.0 4.2 collective-permute-start
  413.7 5.8 collective-permute-done
  423.4 4.2 collective-permute-start
  428.1 4.2 collective-permute-done
  436.3 4.3 collective-permute-start
  441.1 4.3 collective-permute-done
  449.3 5.2 collective-permute-start
  463.0 5.1 collective-permute-start
  475.8 4.7 collective-permute-start
  487.7 11.1 %collective-permute-start = (bf16[512,2,1,128]{3,0,2,1:T(8,128)(2,1)S(1)}, bf16[512,2,1,128]{3,0,2,1:T(8,128)(2,1)S(1)}, u32[]{:S(2)}, u32[]{:S(2)}) collective-permute-start(bf16[512,2,1,128]{3,0,2,1:T(8,128)(2,1)S(1)} %get-tuple-element.421), channel_id=1, source_target_pairs={{0,1},{1,2},{2,3},{3,4},{4,5},{5,6},{6,7},{7,8},{8,9},{9,10},{10,1... | collective-permute-start | bytes 786440 | tf_op jit(solution)/shard_map/while/body/eval_jaxpr/ppermute | solution.py:26
  506.9 5.6 collective-permute-start
  520.2 5.8 collective-permute-start
  534.1 6.3 collective-permute-start
  548.3 70.6 %all-gather.8.cloned.1.call-done = bf16[512,4096]{1,0:T(8,128)(2,1)} async-done(((bf16[8,4096]{1,0:T(8,128)(2,1)}), bf16[512,4096]{1,0:T(8,128)(2,1)}) %all-gather.8.cloned.1.call-update) | async-done | bytes 4194320 | tf_op jit(solution)/shard_map/all_gather | solution.py:131
  618.9 6.5 convolution_convert_fusion
  625.4 101.6 %reduce-scatter.2.cloned.1.call-done = bf16[128,4096]{1,0:T(8,128)(2,1)} async-done(((bf16[512,4096]{1,0:T(8,128)(2,1)}), bf16[128,4096]{1,0:T(8,128)(2,1)}) %reduce-scatter.2.cloned.1.call-update) | async-done | bytes 1048592 | tf_op jit(solution)/shard_map/reduce_scatter | solution.py:132
  (242 shorter events, 137.3 us)
Async XLA Ops:
  6.5 4.1 copy-start.4
  6.5 4.1 copy-start.3
  6.5 5.6 copy-start.5
  6.5 49.5 %all-gather.4.cloned.1.call-start = ((), (), s32[]{:S(2)}) async-start(), calls=%async_computation.1 | async-start | bytes 5242880 | tf_op jit(solution)/shard_map/all_gather | solution.py:57
  10.6 308.3 %all-gather.6.cloned.1.call-start = ((), (), s32[]{:S(2)}) async-start(), calls=%async_computation.2 | async-start | bytes 6389760 | tf_op jit(solution)/shard_map/all_gather | solution.py:15
  11.3 607.6 %all-gather.8.cloned.1.call-start = ((), (), s32[]{:S(2)}) async-start(), calls=%async_computation.3 | async-start | bytes 4259840 | tf_op jit(solution)/shard_map/all_gather | solution.py:131
  12.1 715.0 %reduce-scatter.2.cloned.1.call-start = ((), (), s32[]{:S(2)}) async-start(), calls=%async_computation.4 | async-start | bytes 5242880 | tf_op jit(solution)/shard_map/reduce_scatter | solution.py:132
  331.7 2.3 copy-start.1
  336.1 5.6 collective-permute-start
  345.7 7.6 %collective-permute-start = (bf16[512,2,1,128]{3,0,2,1:T(8,128)(2,1)S(1)}, bf16[512,2,1,128]{3,0,2,1:T(8,128)(2,1)S(1)}, u32[]{:S(2)}, u32[]{:S(2)}) collective-permute-start(bf16[512,2,1,128]{3,0,2,1:T(8,128)(2,1)S(1)} %get-tuple-element.421), channel_id=1, source_target_pairs={{0,1},{1,2},{2,3},{3,4},{4,5},{5,6},{6,7},{7,8},{8,9},{9,10},{10,1... | collective-permute-start | bytes 786440 | tf_op jit(solution)/shard_map/while/body/eval_jaxpr/ppermute | solution.py:26
  357.2 7.1 collective-permute-start
  368.3 7.8 %collective-permute-start = (bf16[512,2,1,128]{3,0,2,1:T(8,128)(2,1)S(1)}, bf16[512,2,1,128]{3,0,2,1:T(8,128)(2,1)S(1)}, u32[]{:S(2)}, u32[]{:S(2)}) collective-permute-start(bf16[512,2,1,128]{3,0,2,1:T(8,128)(2,1)S(1)} %get-tuple-element.421), channel_id=1, source_target_pairs={{0,1},{1,2},{2,3},{3,4},{4,5},{5,6},{6,7},{7,8},{8,9},{9,10},{10,1... | collective-permute-start | bytes 786440 | tf_op jit(solution)/shard_map/while/body/eval_jaxpr/ppermute | solution.py:26
  380.0 10.5 %collective-permute-start = (bf16[512,2,1,128]{3,0,2,1:T(8,128)(2,1)S(1)}, bf16[512,2,1,128]{3,0,2,1:T(8,128)(2,1)S(1)}, u32[]{:S(2)}, u32[]{:S(2)}) collective-permute-start(bf16[512,2,1,128]{3,0,2,1:T(8,128)(2,1)S(1)} %get-tuple-element.421), channel_id=1, source_target_pairs={{0,1},{1,2},{2,3},{3,4},{4,5},{5,6},{6,7},{7,8},{8,9},{9,10},{10,1... | collective-permute-start | bytes 786440 | tf_op jit(solution)/shard_map/while/body/eval_jaxpr/ppermute | solution.py:26
  394.4 10.7 %collective-permute-start = (bf16[512,2,1,128]{3,0,2,1:T(8,128)(2,1)S(1)}, bf16[512,2,1,128]{3,0,2,1:T(8,128)(2,1)S(1)}, u32[]{:S(2)}, u32[]{:S(2)}) collective-permute-start(bf16[512,2,1,128]{3,0,2,1:T(8,128)(2,1)S(1)} %get-tuple-element.421), channel_id=1, source_target_pairs={{0,1},{1,2},{2,3},{3,4},{4,5},{5,6},{6,7},{7,8},{8,9},{9,10},{10,1... | collective-permute-start | bytes 786440 | tf_op jit(solution)/shard_map/while/body/eval_jaxpr/ppermute | solution.py:26
  409.0 10.5 %collective-permute-start = (bf16[512,2,1,128]{3,0,2,1:T(8,128)(2,1)S(1)}, bf16[512,2,1,128]{3,0,2,1:T(8,128)(2,1)S(1)}, u32[]{:S(2)}, u32[]{:S(2)}) collective-permute-start(bf16[512,2,1,128]{3,0,2,1:T(8,128)(2,1)S(1)} %get-tuple-element.421), channel_id=1, source_target_pairs={{0,1},{1,2},{2,3},{3,4},{4,5},{5,6},{6,7},{7,8},{8,9},{9,10},{10,1... | collective-permute-start | bytes 786440 | tf_op jit(solution)/shard_map/while/body/eval_jaxpr/ppermute | solution.py:26
  423.4 8.9 %collective-permute-start = (bf16[512,2,1,128]{3,0,2,1:T(8,128)(2,1)S(1)}, bf16[512,2,1,128]{3,0,2,1:T(8,128)(2,1)S(1)}, u32[]{:S(2)}, u32[]{:S(2)}) collective-permute-start(bf16[512,2,1,128]{3,0,2,1:T(8,128)(2,1)S(1)} %get-tuple-element.421), channel_id=1, source_target_pairs={{0,1},{1,2},{2,3},{3,4},{4,5},{5,6},{6,7},{7,8},{8,9},{9,10},{10,1... | collective-permute-start | bytes 786440 | tf_op jit(solution)/shard_map/while/body/eval_jaxpr/ppermute | solution.py:26
  436.3 9.1 %collective-permute-start = (bf16[512,2,1,128]{3,0,2,1:T(8,128)(2,1)S(1)}, bf16[512,2,1,128]{3,0,2,1:T(8,128)(2,1)S(1)}, u32[]{:S(2)}, u32[]{:S(2)}) collective-permute-start(bf16[512,2,1,128]{3,0,2,1:T(8,128)(2,1)S(1)} %get-tuple-element.421), channel_id=1, source_target_pairs={{0,1},{1,2},{2,3},{3,4},{4,5},{5,6},{6,7},{7,8},{8,9},{9,10},{10,1... | collective-permute-start | bytes 786440 | tf_op jit(solution)/shard_map/while/body/eval_jaxpr/ppermute | solution.py:26
  449.3 9.8 %collective-permute-start = (bf16[512,2,1,128]{3,0,2,1:T(8,128)(2,1)S(1)}, bf16[512,2,1,128]{3,0,2,1:T(8,128)(2,1)S(1)}, u32[]{:S(2)}, u32[]{:S(2)}) collective-permute-start(bf16[512,2,1,128]{3,0,2,1:T(8,128)(2,1)S(1)} %get-tuple-element.421), channel_id=1, source_target_pairs={{0,1},{1,2},{2,3},{3,4},{4,5},{5,6},{6,7},{7,8},{8,9},{9,10},{10,1... | collective-permute-start | bytes 786440 | tf_op jit(solution)/shard_map/while/body/eval_jaxpr/ppermute | solution.py:26
  463.0 8.8 %collective-permute-start = (bf16[512,2,1,128]{3,0,2,1:T(8,128)(2,1)S(1)}, bf16[512,2,1,128]{3,0,2,1:T(8,128)(2,1)S(1)}, u32[]{:S(2)}, u32[]{:S(2)}) collective-permute-start(bf16[512,2,1,128]{3,0,2,1:T(8,128)(2,1)S(1)} %get-tuple-element.421), channel_id=1, source_target_pairs={{0,1},{1,2},{2,3},{3,4},{4,5},{5,6},{6,7},{7,8},{8,9},{9,10},{10,1... | collective-permute-start | bytes 786440 | tf_op jit(solution)/shard_map/while/body/eval_jaxpr/ppermute | solution.py:26
  475.8 8.0 %collective-permute-start = (bf16[512,2,1,128]{3,0,2,1:T(8,128)(2,1)S(1)}, bf16[512,2,1,128]{3,0,2,1:T(8,128)(2,1)S(1)}, u32[]{:S(2)}, u32[]{:S(2)}) collective-permute-start(bf16[512,2,1,128]{3,0,2,1:T(8,128)(2,1)S(1)} %get-tuple-element.421), channel_id=1, source_target_pairs={{0,1},{1,2},{2,3},{3,4},{4,5},{5,6},{6,7},{7,8},{8,9},{9,10},{10,1... | collective-permute-start | bytes 786440 | tf_op jit(solution)/shard_map/while/body/eval_jaxpr/ppermute | solution.py:26
  487.7 15.3 %collective-permute-start = (bf16[512,2,1,128]{3,0,2,1:T(8,128)(2,1)S(1)}, bf16[512,2,1,128]{3,0,2,1:T(8,128)(2,1)S(1)}, u32[]{:S(2)}, u32[]{:S(2)}) collective-permute-start(bf16[512,2,1,128]{3,0,2,1:T(8,128)(2,1)S(1)} %get-tuple-element.421), channel_id=1, source_target_pairs={{0,1},{1,2},{2,3},{3,4},{4,5},{5,6},{6,7},{7,8},{8,9},{9,10},{10,1... | collective-permute-start | bytes 786440 | tf_op jit(solution)/shard_map/while/body/eval_jaxpr/ppermute | solution.py:26
  506.9 9.4 %collective-permute-start = (bf16[512,2,1,128]{3,0,2,1:T(8,128)(2,1)S(1)}, bf16[512,2,1,128]{3,0,2,1:T(8,128)(2,1)S(1)}, u32[]{:S(2)}, u32[]{:S(2)}) collective-permute-start(bf16[512,2,1,128]{3,0,2,1:T(8,128)(2,1)S(1)} %get-tuple-element.421), channel_id=1, source_target_pairs={{0,1},{1,2},{2,3},{3,4},{4,5},{5,6},{6,7},{7,8},{8,9},{9,10},{10,1... | collective-permute-start | bytes 786440 | tf_op jit(solution)/shard_map/while/body/eval_jaxpr/ppermute | solution.py:26
  520.2 9.9 %collective-permute-start = (bf16[512,2,1,128]{3,0,2,1:T(8,128)(2,1)S(1)}, bf16[512,2,1,128]{3,0,2,1:T(8,128)(2,1)S(1)}, u32[]{:S(2)}, u32[]{:S(2)}) collective-permute-start(bf16[512,2,1,128]{3,0,2,1:T(8,128)(2,1)S(1)} %get-tuple-element.421), channel_id=1, source_target_pairs={{0,1},{1,2},{2,3},{3,4},{4,5},{5,6},{6,7},{7,8},{8,9},{9,10},{10,1... | collective-permute-start | bytes 786440 | tf_op jit(solution)/shard_map/while/body/eval_jaxpr/ppermute | solution.py:26
  534.1 9.8 %collective-permute-start = (bf16[512,2,1,128]{3,0,2,1:T(8,128)(2,1)S(1)}, bf16[512,2,1,128]{3,0,2,1:T(8,128)(2,1)S(1)}, u32[]{:S(2)}, u32[]{:S(2)}) collective-permute-start(bf16[512,2,1,128]{3,0,2,1:T(8,128)(2,1)S(1)} %get-tuple-element.421), channel_id=1, source_target_pairs={{0,1},{1,2},{2,3},{3,4},{4,5},{5,6},{6,7},{7,8},{8,9},{9,10},{10,1... | collective-permute-start | bytes 786440 | tf_op jit(solution)/shard_map/while/body/eval_jaxpr/ppermute | solution.py:26
  (2 other events, 2.7 us)
Sparse Core Ops, SparseCore 0:
  10.7 45.2 all-gather.3
  57.8 261.0 all-gather.5
  320.7 298.1 all-gather.7
  625.5 101.4 reduce-scatter.1
where the time goes:
time: 734 us
  waiting for transfers between devices  541 us (74%)
  starting transfers between devices  78.5 us (11%)
  matrix products  63.8 us (9%)
  other arithmetic  32.9 us (4%)
  between operations  13.4 us (2%)
    all_gather x1, waiting for transfers between devices, in_one_piece(): lax.all_gather(both, axis, axis=dim, tiled=True)  263 us
    reduce_scatter x1, waiting for transfers between devices, on_device(): lax.psum_scatter(jnp.dot(mixed, head_rows, preferred_element_type=jnp.flo...  102 us
    ppermute x16, starting transfers between devices, shifted(): lax.ppermute(value, axis, [(source, source + steps) for source in range(f...  78.4 us
    all_gather x1, waiting for transfers between devices, on_device(): head_rows = lax.all_gather(w_out, 'blk', axis=0, tiled=True)  70.6 us
    ppermute x16, waiting for transfers between devices, shifted(): lax.ppermute(value, axis, [(source, source + steps) for source in range(f...  62.8 us
    all_gather x1, waiting for transfers between devices, on_device(): block_input = lax.all_gather(normalized_input, 'heads', axis=0, tiled=True)  42.2 us
    dot_general x17, matrix products, attend_tile(): jnp.einsum('hgqk,khd->hgqd', probs.astype(jnp.bfloat16), kv_now[:, 1], pr...  32.2 us
    reduce_sum x17, other arithmetic, attend_tile(): totals = totals * fading + jnp.sum(probs, axis=-1)  17.7 us
  transfers between devices with their start and end apart: 20, of which 20 were waited for; matrix products, arithmetic and copies ran while one was open for 12% of the time, Pallas kernels for 0%

commit v1 on v0

--- a/solution.py
+++ b/solution.py
@@ -54,7 +54,10 @@
     normalized_input = (
         values * lax.rsqrt(jnp.mean(values * values, axis=1, keepdims=True) + norm_epsilon)
     ).astype(jnp.bfloat16)
-    block_input = lax.all_gather(normalized_input, "heads", axis=0, tiled=True)
+    block_input = jnp.concatenate(
+        lax.all_to_all(jnp.stack([normalized_input] * lax.axis_size("heads")), "heads", 0, 0),
+        axis=0,
+    )
     block_rows = block_input.shape[0]
     query_cols = w_query.shape[1]
     kv_cols = key_value_weight.shape[2]

time: 734 us -> 693 us (0.944)
  waiting for transfers between devices: 541 us -> 479 us
  local copies, waits for them, and re-layouts: 2.52 us -> 15.3 us
  starting transfers between devices: 78.5 us -> 87.8 us
    all_gather x1, waiting for transfers between devices: 263 us -> 192 us  [in_one_piece(): lax.all_gather(both, axis, axis=dim, tiled=True)]
    all_to_all x0 -> x1, waiting for transfers between devices: none -> 59.8 us  [on_device(): lax.all_to_all(jnp.stack([normalized_input] * lax.axis_size('heads')), 'h...]
    all_gather x1 -> x0, waiting for transfers between devices: 42.2 us -> none  [on_device(): block_input = lax.all_gather(normalized_input, 'heads', axis=0, tiled=True)]
    dot_general x0 -> x2, local copies, waits for them, and re-layouts: none -> 10.8 us  [on_device(): jnp.dot(block_input, pieces[0], preferred_element_type=jnp.float32)]
    all_gather x1, waiting for transfers between devices: 70.6 us -> 61.1 us  [on_device(): head_rows = lax.all_gather(w_out, 'blk', axis=0, tiled=True)]
    all_to_all x0 -> x1, starting transfers between devices: none -> 8.13 us  [on_device(): lax.all_to_all(jnp.stack([normalized_input] * lax.axis_size('heads')), 'h...]
  transfers between devices with their start and end apart: 20 -> 20, of which waited for: 20 -> 20; matrix products, arithmetic and copies ran while one was open for 12% -> 15% of each run, Pallas kernels for 0% -> 0%
where the time goes in v1:
time: 693 us; the launch traced here: 692 us
  waiting for transfers between devices  479 us (69%)
  starting transfers between devices  87.8 us (13%)
  matrix products  63.5 us (9%)
  other arithmetic  32 us (5%)
  local copies, waits for them, and re-layouts  15.3 us (2%)
  between operations  13.3 us (2%)
    all_gather x1, waiting for transfers between devices, in_one_piece(): lax.all_gather(both, axis, axis=dim, tiled=True)  192 us
    reduce_scatter x1, waiting for transfers between devices, on_device(): lax.psum_scatter(jnp.dot(mixed, head_rows, preferred_element_type=jnp.flo...  102 us
    ppermute x16, starting transfers between devices, shifted(): lax.ppermute(value, axis, [(source, source + steps) for source in range(f...  79.6 us
    ppermute x16, waiting for transfers between devices, shifted(): lax.ppermute(value, axis, [(source, source + steps) for source in range(f...  64.2 us
    all_gather x1, waiting for transfers between devices, on_device(): head_rows = lax.all_gather(w_out, 'blk', axis=0, tiled=True)  61.1 us
    all_to_all x1, waiting for transfers between devices, on_device(): lax.all_to_all(jnp.stack([normalized_input] * lax.axis_size('heads')), 'h...  59.8 us
    dot_general x17, matrix products, attend_tile(): jnp.einsum('hgqk,khd->hgqd', probs.astype(jnp.bfloat16), kv_now[:, 1], pr...  32.2 us
    reduce_sum x17, other arithmetic, attend_tile(): totals = totals * fading + jnp.sum(probs, axis=-1)  17.7 us
  transfers between devices with their start and end apart: 20, of which 20 were waited for; matrix products, arithmetic and copies ran while one was open for 15% of the time, Pallas kernels for 0%

profile of v1, /device:TPU:1, one launch (start us, length us, event | category | flops | bytes accessed | tf_op | source)
XLA Modules:
  0.0 692.3 jit_solution(11420919164715837436)
XLA Ops:
  14.3 8.1 %all-to-all-start = ((bf16[4,128,4096]{2,1,0:T(8,128)(2,1)}), bf16[4,128,4096]{2,1,0:T(8,128)(2,1)}, u32[]{:S(2)}, u32[]{:S(2)}) async-start(bf16[4,128,4096]{2,1,0:T(8,128)(2,1)} %stack.6), calls=%async_computation | async-start | bytes 8388608 | tf_op jit(solution)/shard_map/all_to_all | solution.py:58
  24.5 59.8 %all-to-all-done = bf16[4,128,4096]{2,1,0:T(8,128)(2,1)} async-done(((bf16[4,128,4096]{2,1,0:T(8,128)(2,1)}), bf16[4,128,4096]{2,1,0:T(8,128)(2,1)}, u32[]{:S(2)}, u32[]{:S(2)}) %all-to-all-start) | async-done | bytes 4194336 | tf_op jit(solution)/shard_map/all_to_all | solution.py:58
  84.3 191.5 %all-gather.3.cloned.1.call-done = bf16[4096,768]{1,0:T(8,128)(2,1)} async-done(((bf16[64,768]{1,0:T(8,128)(2,1)}), bf16[4096,768]{1,0:T(8,128)(2,1)}) %all-gather.3.cloned.1.call-update) | async-done | bytes 6291472 | tf_op jit(solution)/shard_map/all_gather | solution.py:15
  280.8 4.4 slice_bitcast_fusion.4
  285.2 6.4 copy.24
  291.6 5.8 fusion.62
  301.6 214.4 %while.22 = (s32[]{:T(128)}, bf16[512,2,1,128]{3,0,2,1:T(8,128)(2,1)S(1)}, f32[1,4,512]{2,1,0:T(4,128)S(1)}, f32[1,4,512]{2,1,0:T(4,128)S(1)}, f32[1,4,512,128]{...) while((s32[]{:T(128)}, ...), condition=%wide.region_10.11_spmd.clone, body=%wide.region_6.10_spmd.clone.sunk | while | flops 552107520 | bytes 18236672 | solution.py:130
  349.4 7.0 %collective-permute-done = bf16[512,2,1,128]{3,0,2,1:T(8,128)(2,1)S(1)} collective-permute-done((bf16[512,2,1,128]{3,0,2,1:T(8,128)(2,1)S(1)}, bf16[512,2,1,128]{3,0,2,1:T(8,128)(2,1)S(1)}, u32[]{:S(2)}, u32[]{:S(2)}) %collective-permute-start) | collective-permute-done | bytes 262176 | tf_op jit(solution)/shard_map/while/body/eval_jaxpr/ppermute | solution.py:26
  364.9 5.2 collective-permute-done
  374.0 4.2 collective-permute-start
  378.7 4.5 collective-permute-done
  387.1 4.3 collective-permute-start
  399.8 4.6 collective-permute-start
  412.0 8.0 %collective-permute-start = (bf16[512,2,1,128]{3,0,2,1:T(8,128)(2,1)S(1)}, bf16[512,2,1,128]{3,0,2,1:T(8,128)(2,1)S(1)}, u32[]{:S(2)}, u32[]{:S(2)}) collective-permute-start(bf16[512,2,1,128]{3,0,2,1:T(8,128)(2,1)S(1)} %get-tuple-element.419), channel_id=1, source_target_pairs={{0,1},{1,2},{2,3},{3,4},{4,5},{5,6},{6,7},{7,8},{8,9},{9,10},{10,1... | collective-permute-start | bytes 786440 | tf_op jit(solution)/shard_map/while/body/eval_jaxpr/ppermute | solution.py:26
  420.4 5.2 collective-permute-done
  442.2 4.2 collective-permute-start
  453.7 11.6 %collective-permute-start = (bf16[512,2,1,128]{3,0,2,1:T(8,128)(2,1)S(1)}, bf16[512,2,1,128]{3,0,2,1:T(8,128)(2,1)S(1)}, u32[]{:S(2)}, u32[]{:S(2)}) collective-permute-start(bf16[512,2,1,128]{3,0,2,1:T(8,128)(2,1)S(1)} %get-tuple-element.419), channel_id=1, source_target_pairs={{0,1},{1,2},{2,3},{3,4},{4,5},{5,6},{6,7},{7,8},{8,9},{9,10},{10,1... | collective-permute-start | bytes 786440 | tf_op jit(solution)/shard_map/while/body/eval_jaxpr/ppermute | solution.py:26
  465.8 4.6 collective-permute-done
  474.3 5.6 collective-permute-start
  488.0 5.5 collective-permute-start
  501.5 6.6 collective-permute-start
  516.5 61.1 %all-gather.5.cloned.1.call-done = bf16[512,4096]{1,0:T(8,128)(2,1)} async-done(((bf16[8,4096]{1,0:T(8,128)(2,1)}), bf16[512,4096]{1,0:T(8,128)(2,1)}) %all-gather.5.cloned.1.call-update) | async-done | bytes 4194320 | tf_op jit(solution)/shard_map/all_gather | solution.py:134
  577.6 6.5 convolution_convert_fusion
  584.1 101.7 %reduce-scatter.2.cloned.1.call-done = bf16[128,4096]{1,0:T(8,128)(2,1)} async-done(((bf16[512,4096]{1,0:T(8,128)(2,1)}), bf16[128,4096]{1,0:T(8,128)(2,1)}) %reduce-scatter.2.cloned.1.call-update) | async-done | bytes 1048592 | tf_op jit(solution)/shard_map/reduce_scatter | solution.py:135
  (232 shorter events, 151.1 us)
Async XLA Ops:
  6.5 269.3 %all-gather.3.cloned.1.call-start = ((), (), s32[]{:S(2)}) async-start(), calls=%async_computation.2 | async-start | bytes 6389760 | tf_op jit(solution)/shard_map/all_gather | solution.py:15
  14.3 8.9 %copy-start = (s32[16]{0:T(128)S(1)}, s32[16]{0:T(128)}, u32[]{:S(2)}) copy-start(s32[16]{0:T(128)} %param.11) | copy-start | bytes 196
  14.3 70.0 %all-to-all-start = ((bf16[4,128,4096]{2,1,0:T(8,128)(2,1)}), bf16[4,128,4096]{2,1,0:T(8,128)(2,1)}, u32[]{:S(2)}, u32[]{:S(2)}) async-start(bf16[4,128,4096]{2,1,0:T(8,128)(2,1)} %stack.6), calls=%async_computation | async-start | bytes 8388608 | tf_op jit(solution)/shard_map/all_to_all | solution.py:58
  22.5 555.1 %all-gather.5.cloned.1.call-start = ((), (), s32[]{:S(2)}) async-start(), calls=%async_computation.3 | async-start | bytes 4259840 | tf_op jit(solution)/shard_map/all_gather | solution.py:134
  23.2 662.6 %reduce-scatter.2.cloned.1.call-start = ((), (), s32[]{:S(2)}) async-start(), calls=%async_computation.4 | async-start | bytes 5242880 | tf_op jit(solution)/shard_map/reduce_scatter | solution.py:135
  301.6 5.3 collective-permute-start
  310.8 7.3 %collective-permute-start = (bf16[512,2,1,128]{3,0,2,1:T(8,128)(2,1)S(1)}, bf16[512,2,1,128]{3,0,2,1:T(8,128)(2,1)S(1)}, u32[]{:S(2)}, u32[]{:S(2)}) collective-permute-start(bf16[512,2,1,128]{3,0,2,1:T(8,128)(2,1)S(1)} %get-tuple-element.419), channel_id=1, source_target_pairs={{0,1},{1,2},{2,3},{3,4},{4,5},{5,6},{6,7},{7,8},{8,9},{9,10},{10,1... | collective-permute-start | bytes 786440 | tf_op jit(solution)/shard_map/while/body/eval_jaxpr/ppermute | solution.py:26
  322.0 7.1 %collective-permute-start = (bf16[512,2,1,128]{3,0,2,1:T(8,128)(2,1)S(1)}, bf16[512,2,1,128]{3,0,2,1:T(8,128)(2,1)S(1)}, u32[]{:S(2)}, u32[]{:S(2)}) collective-permute-start(bf16[512,2,1,128]{3,0,2,1:T(8,128)(2,1)S(1)} %get-tuple-element.419), channel_id=1, source_target_pairs={{0,1},{1,2},{2,3},{3,4},{4,5},{5,6},{6,7},{7,8},{8,9},{9,10},{10,1... | collective-permute-start | bytes 786440 | tf_op jit(solution)/shard_map/while/body/eval_jaxpr/ppermute | solution.py:26
  333.0 8.1 %collective-permute-start = (bf16[512,2,1,128]{3,0,2,1:T(8,128)(2,1)S(1)}, bf16[512,2,1,128]{3,0,2,1:T(8,128)(2,1)S(1)}, u32[]{:S(2)}, u32[]{:S(2)}) collective-permute-start(bf16[512,2,1,128]{3,0,2,1:T(8,128)(2,1)S(1)} %get-tuple-element.419), channel_id=1, source_target_pairs={{0,1},{1,2},{2,3},{3,4},{4,5},{5,6},{6,7},{7,8},{8,9},{9,10},{10,1... | collective-permute-start | bytes 786440 | tf_op jit(solution)/shard_map/while/body/eval_jaxpr/ppermute | solution.py:26
  345.1 11.3 %collective-permute-start = (bf16[512,2,1,128]{3,0,2,1:T(8,128)(2,1)S(1)}, bf16[512,2,1,128]{3,0,2,1:T(8,128)(2,1)S(1)}, u32[]{:S(2)}, u32[]{:S(2)}) collective-permute-start(bf16[512,2,1,128]{3,0,2,1:T(8,128)(2,1)S(1)} %get-tuple-element.419), channel_id=1, source_target_pairs={{0,1},{1,2},{2,3},{3,4},{4,5},{5,6},{6,7},{7,8},{8,9},{9,10},{10,1... | collective-permute-start | bytes 786440 | tf_op jit(solution)/shard_map/while/body/eval_jaxpr/ppermute | solution.py:26
  360.3 9.8 %collective-permute-start = (bf16[512,2,1,128]{3,0,2,1:T(8,128)(2,1)S(1)}, bf16[512,2,1,128]{3,0,2,1:T(8,128)(2,1)S(1)}, u32[]{:S(2)}, u32[]{:S(2)}) collective-permute-start(bf16[512,2,1,128]{3,0,2,1:T(8,128)(2,1)S(1)} %get-tuple-element.419), channel_id=1, source_target_pairs={{0,1},{1,2},{2,3},{3,4},{4,5},{5,6},{6,7},{7,8},{8,9},{9,10},{10,1... | collective-permute-start | bytes 786440 | tf_op jit(solution)/shard_map/while/body/eval_jaxpr/ppermute | solution.py:26
  374.0 9.2 %collective-permute-start = (bf16[512,2,1,128]{3,0,2,1:T(8,128)(2,1)S(1)}, bf16[512,2,1,128]{3,0,2,1:T(8,128)(2,1)S(1)}, u32[]{:S(2)}, u32[]{:S(2)}) collective-permute-start(bf16[512,2,1,128]{3,0,2,1:T(8,128)(2,1)S(1)} %get-tuple-element.419), channel_id=1, source_target_pairs={{0,1},{1,2},{2,3},{3,4},{4,5},{5,6},{6,7},{7,8},{8,9},{9,10},{10,1... | collective-permute-start | bytes 786440 | tf_op jit(solution)/shard_map/while/body/eval_jaxpr/ppermute | solution.py:26
  387.1 8.8 %collective-permute-start = (bf16[512,2,1,128]{3,0,2,1:T(8,128)(2,1)S(1)}, bf16[512,2,1,128]{3,0,2,1:T(8,128)(2,1)S(1)}, u32[]{:S(2)}, u32[]{:S(2)}) collective-permute-start(bf16[512,2,1,128]{3,0,2,1:T(8,128)(2,1)S(1)} %get-tuple-element.419), channel_id=1, source_target_pairs={{0,1},{1,2},{2,3},{3,4},{4,5},{5,6},{6,7},{7,8},{8,9},{9,10},{10,1... | collective-permute-start | bytes 786440 | tf_op jit(solution)/shard_map/while/body/eval_jaxpr/ppermute | solution.py:26
  399.8 8.2 %collective-permute-start = (bf16[512,2,1,128]{3,0,2,1:T(8,128)(2,1)S(1)}, bf16[512,2,1,128]{3,0,2,1:T(8,128)(2,1)S(1)}, u32[]{:S(2)}, u32[]{:S(2)}) collective-permute-start(bf16[512,2,1,128]{3,0,2,1:T(8,128)(2,1)S(1)} %get-tuple-element.419), channel_id=1, source_target_pairs={{0,1},{1,2},{2,3},{3,4},{4,5},{5,6},{6,7},{7,8},{8,9},{9,10},{10,1... | collective-permute-start | bytes 786440 | tf_op jit(solution)/shard_map/while/body/eval_jaxpr/ppermute | solution.py:26
  412.0 13.6 %collective-permute-start = (bf16[512,2,1,128]{3,0,2,1:T(8,128)(2,1)S(1)}, bf16[512,2,1,128]{3,0,2,1:T(8,128)(2,1)S(1)}, u32[]{:S(2)}, u32[]{:S(2)}) collective-permute-start(bf16[512,2,1,128]{3,0,2,1:T(8,128)(2,1)S(1)} %get-tuple-element.419), channel_id=1, source_target_pairs={{0,1},{1,2},{2,3},{3,4},{4,5},{5,6},{6,7},{7,8},{8,9},{9,10},{10,1... | collective-permute-start | bytes 786440 | tf_op jit(solution)/shard_map/while/body/eval_jaxpr/ppermute | solution.py:26
  429.5 8.8 %collective-permute-start = (bf16[512,2,1,128]{3,0,2,1:T(8,128)(2,1)S(1)}, bf16[512,2,1,128]{3,0,2,1:T(8,128)(2,1)S(1)}, u32[]{:S(2)}, u32[]{:S(2)}) collective-permute-start(bf16[512,2,1,128]{3,0,2,1:T(8,128)(2,1)S(1)} %get-tuple-element.419), channel_id=1, source_target_pairs={{0,1},{1,2},{2,3},{3,4},{4,5},{5,6},{6,7},{7,8},{8,9},{9,10},{10,1... | collective-permute-start | bytes 786440 | tf_op jit(solution)/shard_map/while/body/eval_jaxpr/ppermute | solution.py:26
  442.2 7.6 %collective-permute-start = (bf16[512,2,1,128]{3,0,2,1:T(8,128)(2,1)S(1)}, bf16[512,2,1,128]{3,0,2,1:T(8,128)(2,1)S(1)}, u32[]{:S(2)}, u32[]{:S(2)}) collective-permute-start(bf16[512,2,1,128]{3,0,2,1:T(8,128)(2,1)S(1)} %get-tuple-element.419), channel_id=1, source_target_pairs={{0,1},{1,2},{2,3},{3,4},{4,5},{5,6},{6,7},{7,8},{8,9},{9,10},{10,1... | collective-permute-start | bytes 786440 | tf_op jit(solution)/shard_map/while/body/eval_jaxpr/ppermute | solution.py:26
  453.7 16.6 %collective-permute-start = (bf16[512,2,1,128]{3,0,2,1:T(8,128)(2,1)S(1)}, bf16[512,2,1,128]{3,0,2,1:T(8,128)(2,1)S(1)}, u32[]{:S(2)}, u32[]{:S(2)}) collective-permute-start(bf16[512,2,1,128]{3,0,2,1:T(8,128)(2,1)S(1)} %get-tuple-element.419), channel_id=1, source_target_pairs={{0,1},{1,2},{2,3},{3,4},{4,5},{5,6},{6,7},{7,8},{8,9},{9,10},{10,1... | collective-permute-start | bytes 786440 | tf_op jit(solution)/shard_map/while/body/eval_jaxpr/ppermute | solution.py:26
  474.3 9.8 %collective-permute-start = (bf16[512,2,1,128]{3,0,2,1:T(8,128)(2,1)S(1)}, bf16[512,2,1,128]{3,0,2,1:T(8,128)(2,1)S(1)}, u32[]{:S(2)}, u32[]{:S(2)}) collective-permute-start(bf16[512,2,1,128]{3,0,2,1:T(8,128)(2,1)S(1)} %get-tuple-element.419), channel_id=1, source_target_pairs={{0,1},{1,2},{2,3},{3,4},{4,5},{5,6},{6,7},{7,8},{8,9},{9,10},{10,1... | collective-permute-start | bytes 786440 | tf_op jit(solution)/shard_map/while/body/eval_jaxpr/ppermute | solution.py:26
  488.0 9.6 %collective-permute-start = (bf16[512,2,1,128]{3,0,2,1:T(8,128)(2,1)S(1)}, bf16[512,2,1,128]{3,0,2,1:T(8,128)(2,1)S(1)}, u32[]{:S(2)}, u32[]{:S(2)}) collective-permute-start(bf16[512,2,1,128]{3,0,2,1:T(8,128)(2,1)S(1)} %get-tuple-element.419), channel_id=1, source_target_pairs={{0,1},{1,2},{2,3},{3,4},{4,5},{5,6},{6,7},{7,8},{8,9},{9,10},{10,1... | collective-permute-start | bytes 786440 | tf_op jit(solution)/shard_map/while/body/eval_jaxpr/ppermute | solution.py:26
  501.5 10.4 %collective-permute-start = (bf16[512,2,1,128]{3,0,2,1:T(8,128)(2,1)S(1)}, bf16[512,2,1,128]{3,0,2,1:T(8,128)(2,1)S(1)}, u32[]{:S(2)}, u32[]{:S(2)}) collective-permute-start(bf16[512,2,1,128]{3,0,2,1:T(8,128)(2,1)S(1)} %get-tuple-element.419), channel_id=1, source_target_pairs={{0,1},{1,2},{2,3},{3,4},{4,5},{5,6},{6,7},{7,8},{8,9},{9,10},{10,1... | collective-permute-start | bytes 786440 | tf_op jit(solution)/shard_map/while/body/eval_jaxpr/ppermute | solution.py:26
Sparse Core Ops, SparseCore 0:
  9.1 266.6 all-gather.2
  277.6 299.9 all-gather.4
  584.2 101.5 reduce-scatter.1
